TPU v7x, 16 devices: a whole 2x2x2 slice. The times are simulated.
16 devices in a mesh: rep: 1, dp: 16 (over x, y, z, core).
Axes of the slice: x: 2, y: 2, z: 2, core: 2. Of those that a mesh axis runs over, the one named last changes fastest.
Arguments:
- g_w_gate: bfloat16 [16, 2, 1024, 2816], P(('rep', 'dp'))
- g_w_up: bfloat16 [16, 2, 1024, 2816], P(('rep', 'dp'))
- g_w_down: bfloat16 [16, 2, 2816, 1024], P(('rep', 'dp'))
- w_gate: bfloat16 [2, 1024, 2816], replicated
- w_up: bfloat16 [2, 1024, 2816], replicated
- w_down: bfloat16 [2, 2816, 1024], replicated
- m_w_gate: float32 [2, 1024, 2816], P(None, 'dp')
- m_w_up: float32 [2, 1024, 2816], P(None, 'dp')
- m_w_down: float32 [2, 2816, 1024], P(None, 'dp')
- v_w_gate: float32 [2, 1024, 2816], P(None, 'dp')
- v_w_up: float32 [2, 1024, 2816], P(None, 'dp')
- v_w_down: float32 [2, 2816, 1024], P(None, 'dp')
Outputs:
- output 1: bfloat16 [2, 1024, 2816], P('rep')
- output 2: bfloat16 [2, 1024, 2816], P('rep')
- output 3: bfloat16 [2, 2816, 1024], P('rep')
- output 4: float32 [2, 1024, 2816], P('rep', 'dp')
- output 5: float32 [2, 1024, 2816], P('rep', 'dp')
- output 6: float32 [2, 2816, 1024], P('rep', 'dp')
- output 7: float32 [2, 1024, 2816], P('rep', 'dp')
- output 8: float32 [2, 1024, 2816], P('rep', 'dp')
- output 9: float32 [2, 2816, 1024], P('rep', 'dp')
All inputs are finite; a program needn't handle non-finite values.
Results may differ from a plain program's by a relative error of at most 0.022.
Values are sent between devices in bfloat16 or wider.
A program may use at most 2 GiB of HBM per device.

v0:
```python
import jax
import jax.numpy as jnp
from jax import lax
from jax.experimental import pallas as pl
from jax.experimental.pallas import tpu as pltpu
from jax.sharding import PartitionSpec as P


BF16, F32 = jnp.bfloat16, jnp.float32
MESH = pl.DeviceIdType.MESH
LAYERS = 2
ORDERS = ((0, 1, 2), (1, 2, 0), (2, 0, 1))
STRIDES = (8, 4, 2)
SLAB = 16
EVERY = slice(None)
GRID = (LAYERS, 2, 2, 2, 2)
GRANT = 17 * 1024 * 1024
PARTS = (16, 16, 48)
PIECES = ((0, 0, 0, 1), (1, 0, 1, 2), (2, 1, 0, 2))
PUT_FLOPS = 200_000_000


def adamw(w, m, v, g):
    m = 0.9 * m + 0.1 * g
    v = 0.95 * v + 0.05 * g * g
    step = m * lax.rsqrt(v + 1e-8) + 0.1 * w
    return (w - 0.02 * step).astype(BF16), m, v


class Weight:
    def __init__(self, order, where, core, **refs):
        self.order, self.core = order, core
        self.mine = [where[axis] for axis in order]
        self.__dict__.update(refs)

    def place(self, *stages):
        xyz = [None] * 3
        for axis, coordinate in zip(self.order, stages, strict=True):
            xyz[axis] = coordinate
        return tuple(xyz)

    def own(self):
        return self.block(1, 1, 1)

    def far(self):
        return self.block(0, 0, 0)

    def block(self, keep1, keep2, keep3):
        return self.place(*(1 - m + k * (2 * m - 1) for m, k in zip(self.mine, (keep1, keep2, keep3), strict=True)))


def kernel(*refs):
    threes = (refs[i : i + 3] for i in range(0, 39, 3))
    g_refs, w_refs, m_refs, v_refs, all_refs, m_outs, v_outs, late_refs, mid_refs, firsts, seconds, thirds, olds = threes
    load_sem, pair_sem, rest_sem, s1_sem, s2_sem, s3_sem, a3_sem, a2_sem, a1_sem, last_sem, own_sem, a0_sem, all_send, send_sem, third_sem, free_sem, third_free, read_sem = refs[39:]

    me = lax.axis_index("dp")
    core = me % 2
    where = [(me // s) % 2 for s in STRIDES]
    partners = [me + s * (1 - 2 * b) for s, b in zip(STRIDES, where, strict=True)]
    pair = me + 1 - 2 * core

    weights = [
        Weight(
            ORDERS[i], where, core, i=i, part=PARTS[i], rows=olds[i].shape[1], g=g_refs[i], all=all_refs[i], m=m_outs[i], v=v_outs[i],
            first=firsts[i], second=seconds[i], third=thirds[i], old=olds[i], late=late_refs[i], mid=mid_refs[i],
            to=[partners[axis] for axis in ORDERS[i]],
        )
        for i in range(3)
    ]

    def remote(src, dst, send, recv, device):
        return pltpu.make_async_remote_copy(
            src_ref=src, dst_ref=dst, send_sem=send, recv_sem=recv, device_id={"dp": device}, device_id_type=MESH
        )

    gate = weights[0]
    like = {
        2: gate.third,
        6: gate.first.at[pl.ds(0, 6)],
        8: gate.first,
        12: gate.all.at[:, :, :, :, 0, pl.ds(0, 48)],
        16: gate.all.at[:, :, :, :, 0],
        24: gate.all.at[:, :, :, :, :, pl.ds(0, 48)],
    }

    def sent(sem, ref):
        remote(ref, ref, sem, own_sem, pair).wait_send()

    def received(sem, ref):
        remote(ref, ref, own_sem, sem, pair).wait_recv()

    def loaded(n, ref):
        pltpu.make_async_copy(ref, ref, load_sem.at[n]).wait()

    def unit(w, keep1, k):
        return (k % 2, *w.block(keep1, k // 4, (k // 2) % 2))

    def stage(w):
        return pltpu.make_async_copy(w.g.at[(EVERY, *w.far(), 1 - core)], w.old, load_sem.at[0])

    def load(w, n):
        m2, m3 = w.mine[1:]
        at = (EVERY, *w.place(1 - w.mine[0], *((1 - m2, 1 - m3), (1 - m2, m3), (m2, EVERY))[n]), core)
        return pltpu.make_async_copy(w.g.at[at], w.all.at[at], load_sem.at[(1, 2, 7)[n]])

    def load_rest(w):
        at = (EVERY, *w.place(w.mine[0], EVERY, EVERY), core)
        return pltpu.make_async_copy(w.g.at[at], w.all.at[at], load_sem.at[3])

    def load_m(w):
        return pltpu.make_async_copy(m_refs[w.i], w.m, load_sem.at[4])

    def load_v(w):
        return pltpu.make_async_copy(v_refs[w.i], w.v, load_sem.at[5])

    def load_w(w):
        return pltpu.make_async_copy(w_refs[w.i].at[(EVERY, *w.own(), core)], w.old, load_sem.at[6])

    def to_pair(w, keep1, k, recv=None):
        at, recv = unit(w, keep1, k), rest_sem if keep1 else pair_sem.at[w.i, recv]
        return remote(w.g.at[(*at, 1 - core)], w.all.at[(*at, core)], send_sem.at[w.i, 0], recv, pair)

    def staged_to_pair(w, k, lo, n, recv):
        rows = pl.ds(lo, n)
        return remote(
            w.old.at[k, rows], w.all.at[(*unit(w, 0, k), core, rows)], send_sem.at[w.i, 0], pair_sem.at[w.i, recv], pair
        )

    def first(w, k, lo=0, n=None):
        rows = pl.ds(lo, w.rows if n is None else n)
        at = (*unit(w, 0, k), core, rows)
        return remote(w.all.at[at], w.first.at[k, rows], all_send.at[0], s1_sem.at[k // 2], w.to[0])

    def second(w, k):
        at = (k % 2, *w.block(1, 0, k // 2))
        return remote(w.all.at[(*at, core)], w.second.at[k], all_send.at[1], s2_sem.at[k // 2], w.to[1])

    def third(w, k):
        at = (k, *w.block(1, 1, 0))
        return remote(w.all.at[(*at, core)], w.third.at[k], third_sem.at[w.i, k], s3_sem.at[w.i, k], w.to[2])

    def tell(n, stage):
        for w in weights:
            pl.semaphore_signal(free_sem.at[n], inc=1, device_id={"dp": w.to[stage]}, device_id_type=MESH)

    def told(n):
        pl.semaphore_wait(free_sem.at[n], 3)

    def gather3(w, k):
        at = (k, *w.own(), core)
        return remote(w.all.at[at], w.all.at[at], all_send.at[2], a3_sem, w.to[2])

    def gather2(w, k):
        at = (k % 2, *w.block(1, 1, 1 - k // 2), core)
        return remote(w.all.at[at], w.all.at[at], all_send.at[3], a2_sem.at[k // 2], w.to[1])

    def came(w, keep1, k, lo, n):
        return (k % 2, *w.block(keep1, 1 - k // 4, 1 - (k // 2) % 2), core, pl.ds(lo, w.rows if n is None else n))

    def gather1(w, k, recv, lo=0, n=None):
        at = came(w, 1, k, lo, n)
        sem = a1_sem.at[recv] if recv < 2 else last_sem.at[w.i, recv - 2]
        return remote(w.all.at[at], w.all.at[at], send_sem.at[w.i, 1], sem, w.to[0])

    def gather0(w, keep1, k, lo=0, n=None):
        at = came(w, keep1, k, lo, n)
        send, recv = (all_send.at[4], own_sem) if keep1 else (all_send.at[5], a0_sem)
        return remote(w.all.at[at], w.all.at[at], send, recv, pair)

    def keep_late(w):
        at = (EVERY, *w.block(1, 0, 0), core)
        return pltpu.make_async_copy(w.all.at[at], w.late, load_sem.at[0])

    def keep_mid(w, k, lo, n):
        rows = pl.ds(lo, n)
        return pltpu.make_async_copy(w.all.at[(k, *w.block(0, 0, 1), core, rows)], w.mid.at[k, rows], load_sem.at[1])

    def total(w, at, rows, *others):
        sum_ = w.all[(*at, core, rows, EVERY)].astype(F32) + w.all[(*at, 1 - core, rows, EVERY)].astype(F32)
        for other, k in others:
            sum_ = sum_ + other[k, rows, :].astype(F32)
        return sum_

    def slabs(lo, n, body):
        @pl.loop(0, n // SLAB)
        def _(r):
            body(pl.ds(pl.multiple_of(lo + r * SLAB, SLAB), SLAB))

    def add(w, at, *others, lo=0, n=None):
        def body(rows):
            w.all[(*at, core, rows, EVERY)] = total(w, at, rows, *others).astype(BF16)

        slabs(lo, w.rows if n is None else n, body)

    def each(lo, hi, body):
        @pl.loop(lo, hi)
        def _(k):
            body(k)

    for w in weights:
        stage(w).start()
    for w in weights:
        load(w, 0).start()

    barrier = pltpu.get_barrier_semaphore()
    for device in (pair, *partners):
        pl.semaphore_signal(barrier, inc=1, device_id={"dp": device}, device_id_type=MESH)
    loaded(0, like[6])
    pl.semaphore_wait(barrier, 4)

    for w in weights:
        staged_to_pair(w, 0, 0, w.part, 0).start()
    for w in weights:
        staged_to_pair(w, 0, w.part, w.rows - w.part, 1).start()
    for w in weights:
        staged_to_pair(w, 1, 0, w.rows, 2).start()

    def early(pieces, send):
        for recv, k, begin, end in pieces:
            for w in weights:
                edges = (0, w.part, w.rows)
                lo, n = edges[begin], edges[end] - edges[begin]
                received(pair_sem.at[w.i, recv], w.old.at[0, pl.ds(0, n)])
                add(w, unit(w, 0, k), lo=lo, n=n)
                if send:
                    first(w, k, lo, n).start()

    def start_pair(k, recv):
        for w in weights:
            to_pair(w, 0, k, recv).start()

    def start_pair_rest(k):
        for w in weights:
            to_pair(w, 1, k).start()

    def sum1(k):
        for w in weights:
            add(w, unit(w, 0, k))

    def send1(k):
        for w in weights:
            first(w, k).start()

    def stage1(k):
        sum1(k)
        send1(k)

    loaded(1, like[6])

    @pl.when(core == 0)
    def _():
        early(PIECES[:1], True)

    each(2, 4, lambda k: start_pair(k, 3))
    each(4, 8, lambda k: start_pair(k, 4))
    for n in (1, 2):
        for w in weights:
            load(w, n).start()

    @pl.when(core == 0)
    def _():
        early(PIECES[1:], True)

    each(0, 8, start_pair_rest)
    for w in weights:
        load_rest(w).start()
    loaded(2, like[6])

    @pl.when(core == 1)
    def _():
        early(PIECES, False)
        for w in weights:
            received(pair_sem.at[w.i, 3], w.old)
        each(2, 4, sum1)
        each(0, 4, send1)

    @pl.when(core == 0)
    def _():
        for w in weights:
            received(pair_sem.at[w.i, 3], w.old)
        each(2, 4, stage1)

    loaded(7, like[12])
    for w in weights:
        received(pair_sem.at[w.i, 4], w.second)
    each(4, 8, stage1)
    for w in weights:
        load_m(w).start()
        load_v(w).start()
    loaded(3, like[24])
    received(rest_sem, like[24])
    for w in weights:
        sent(send_sem.at[w.i, 0], like[16])
        load_w(w).start()

    def stage2(k):
        for w in weights:
            add(w, unit(w, 1, k), (w.first, k))
        for w in weights:
            second(w, k).start()

    for n in (0, 1):
        received(s1_sem.at[n], like[6])
        each(2 * n, 2 * n + 2, stage2)

    def stage3(k):
        for w in weights:
            add(w, unit(w, 1, 4 + k), (w.first, 4 + k), (w.second, k))
        for w in weights:
            third(w, k).start()

    received(s1_sem.at[2], like[6])
    received(s2_sem.at[0], like[6])
    each(0, 2, stage3)
    loaded(4, like[12])
    loaded(5, like[12])
    loaded(6, like[6])
    sent(all_send.at[0], like[24])
    tell(0, 0)
    received(s1_sem.at[3], like[6])
    sent(all_send.at[1], like[12])
    tell(1, 1)
    received(s2_sem.at[1], like[6])

    def update(k):
        for w in weights:
            third(w, k).wait()
            pl.semaphore_signal(third_free.at[w.i], inc=1, device_id={"dp": w.to[2]}, device_id_type=MESH)
            at = (k, *w.own())

            def body(rows, w=w, at=at):
                g = total(w, at, rows, (w.first, 6 + k), (w.second, 2 + k), (w.third, k)).astype(BF16).astype(F32)
                new, m, v = adamw(w.old[k, rows, :].astype(F32), w.m[k, rows, :], w.v[k, rows, :], g)
                w.m[k, rows, :] = m
                w.v[k, rows, :] = v
                w.all[(*at, core, rows, EVERY)] = new

            slabs(0, w.rows, body)

        for w in weights:
            pl.semaphore_wait(third_free.at[w.i], 1)
            gather3(w, k).start()

    each(0, 2, update)

    def own21(k):
        for w in weights:
            gather2(w, k).start()
        for w in weights:
            gather1(w, k, 0).start()

    told(1)
    told(0)
    each(0, 2, own21)

    pl.semaphore_signal(read_sem, inc=1, device_id={"dp": pair}, device_id_type=MESH)
    pl.semaphore_wait(read_sem, 1)

    def own0(k):
        for w in weights:
            gather0(w, 1, k).start()

    each(0, 2, own0)

    def back3(k):
        for w in weights:
            gather2(w, 2 + k).start()
        for w in weights:
            gather1(w, 2 + k, 1).start()
            gather0(w, 1, 2 + k).start()

    received(a3_sem, like[6])
    each(0, 2, back3)

    def back2(k):
        for w in weights:
            gather0(w, 1, k).start()

    received(a2_sem.at[0], like[6])
    for w in weights:
        gather1(w, 4, 2).start()
    for w in weights:
        gather1(w, 5, 3, 0, w.rows - w.part).start()
    for w in weights:
        gather1(w, 5, 4, w.rows - w.part, w.part).start()
    each(4, 6, back2)
    received(a2_sem.at[1], like[6])
    for w in weights:
        keep_late(w).start()
    each(6, 8, back2)

    def back1(k):
        for w in weights:
            gather0(w, 0, k).start()

    for n in (0, 1):
        received(a1_sem.at[n], like[6])
        each(2 * n, 2 * n + 2, back1)
    for w in weights:
        received(last_sem.at[w.i, 0], w.third.at[0])
        keep_mid(w, 0, 0, w.rows).start()
    for w in weights:
        received(last_sem.at[w.i, 1], w.third.at[0, pl.ds(0, w.rows - w.part)])
        keep_mid(w, 1, 0, w.rows - w.part).start()
    for w in weights:
        received(last_sem.at[w.i, 2], w.third.at[0, pl.ds(0, w.part)])
        keep_mid(w, 1, w.rows - w.part, w.part).start()

    loaded(0, like[6])
    for n, units in ((2, 6), (3, 12), (4, 24), (5, 12)):
        sent(all_send.at[n], like[units])
    received(own_sem, like[24])
    received(a0_sem, like[12])
    for w in weights:
        sent(send_sem.at[w.i, 1], like[6])
    loaded(1, like[6])


def blocks_of(i):
    me = lax.axis_index("dp")
    return Weight(ORDERS[i], [(me // s) % 2 for s in STRIDES], me % 2)


def run(copies):
    for copy in copies:
        copy.start()
    for copy in copies:
        copy.wait()


def put(*refs):
    ins, outs, sem = refs[:6], refs[6:12], refs[12]
    copies = []
    for i in range(3):
        w = blocks_of(i)
        here, every = w.own(), EVERY
        coordinates = [here[axis] for axis in w.order]
        for n, at in enumerate((
            (every, *w.place(coordinates[0], every, every)),
            (every, *w.place(1 - coordinates[0], coordinates[1], every)),
            (every, *w.block(0, 0, 1), w.core),
        )):
            copies.append(pltpu.make_async_copy(ins[i].at[at], outs[i].at[at], sem.at[i, n]))
        for k in range(LAYERS):
            copies.append(pltpu.make_async_copy(ins[3 + i].at[k], outs[3 + i].at[k], sem.at[3 + i, k]))
    run(copies)


def patch_mid(*refs):
    mids, outs, sem = refs[3:6], refs[6:9], refs[-1]
    copies = []
    for i in range(3):
        w = blocks_of(i)
        copies.append(pltpu.make_async_copy(mids[i], outs[i].at[(EVERY, *w.block(0, 0, 1), 1 - w.core)], sem.at[i]))
    run(copies)


def patch0(*refs):
    _, lates, vs, outs, v_outs = (refs[i : i + 3] for i in range(0, 15, 3))
    sem = refs[-1]
    copies = []
    for i in range(3):
        w = blocks_of(i)
        copies.append(pltpu.make_async_copy(lates[i], outs[i].at[(EVERY, *w.far(), w.core)], sem.at[i, 0]))
        copies.append(pltpu.make_async_copy(vs[i], v_outs[i], sem.at[i, 1]))
    run(copies)


def patch1(*refs):
    theirs, outs, sem = refs[3:6], refs[6:9], refs[-1]
    copies = []
    for i in range(3):
        w = blocks_of(i)
        copies.append(pltpu.make_async_copy(theirs[i], outs[i].at[(EVERY, *w.far(), 1 - w.core)], sem.at[i]))
    run(copies)


def local(kernel_, outs, hbm, vmem, sems, cost=None):
    return list(
        pl.pallas_call(
            kernel_,
            out_shape=[jax.ShapeDtypeStruct(o.shape, o.dtype) for o in outs],
            in_specs=[pl.BlockSpec(memory_space=pl.ANY)] * len(hbm) + [pl.BlockSpec(memory_space=pltpu.VMEM)] * len(vmem),
            out_specs=[pl.BlockSpec(memory_space=pl.ANY)] * len(outs),
            input_output_aliases={j: j for j in range(len(hbm))},
            scratch_shapes=[pltpu.SemaphoreType.DMA(sems)],
            compiler_params=pltpu.CompilerParams(vmem_limit_bytes=GRANT),
            cost_estimate=cost,
        )(*hbm, *(pltpu.with_memory_space_constraint(o, pltpu.VMEM) for o in vmem))
    )


def solution(mesh):
    def whole_step(*arrays):
        shapes = [a.shape[1:] for a in arrays[6:9]]

        def cut(a, i):
            return a.reshape(*GRID, *shapes[i])

        operands = [cut(a, n % 3) for n, a in enumerate(arrays[:6])] + list(arrays[6:])
        blocks = [(n, rows, columns) for n in (8, 4, 2, LAYERS) for rows, columns in shapes]
        outs = pl.pallas_call(
            kernel,
            out_shape=[pltpu.VMEM((*GRID, *s), BF16) for s in shapes] + [pltpu.VMEM((LAYERS, *s), F32) for s in shapes] * 2 + [jax.ShapeDtypeStruct((LAYERS, *s), BF16) for s in shapes] * 2,
            in_specs=[pl.BlockSpec(memory_space=pl.ANY)] * 12,
            out_specs=[pl.BlockSpec(memory_space=pltpu.VMEM)] * 9 + [pl.BlockSpec(memory_space=pl.ANY)] * 6,
            scratch_shapes=[
                *(pltpu.VMEM(s, BF16) for s in blocks),
                *(pltpu.SemaphoreType.DMA(n) for n in ((8,), (3, 5), (), (4,), (2,), (3, 2), (), (2,), (2,), (3, 3), (), (), (6,), (3, 2), (3, 2))),
                *(pltpu.SemaphoreType.REGULAR(n) for n in ((2,), (3,), ())),
            ],
            compiler_params=pltpu.CompilerParams(collective_id=0, has_side_effects=True, vmem_limit_bytes=GRANT),
            name="step",
        )(*operands)

        def axis(i):
            return lax.ppermute(outs[9 + i], "dp", [(d, d ^ STRIDES[ORDERS[i][0]]) for d in range(16)])

        def over(o):
            return lax.ppermute(o, "dp", [(d, d ^ 1) for d in range(16)])

        late = [axis(i) for i in range(3)]
        mids = [over(o) for o in outs[12:]]
        cost = pl.CostEstimate(flops=PUT_FLOPS, bytes_accessed=2 * 32_000_000, transcendentals=0)
        done = local(put, outs[:6], [], outs[:6], (6, 3), cost)
        for i in range(3):
            late[i], done[3 + i] = lax.optimization_barrier((late[i], done[3 + i]))
        theirs = [over(late[i]) for i in range(2)]
        some = local(patch_mid, done[:3], done[:3], mids, (3,))
        late[2], some[0] = lax.optimization_barrier((late[2], some[0]))
        theirs.append(over(late[2]))
        some = local(patch0, some + list(outs[6:9]), some, [*late, *outs[6:9]], (3, 2))
        weights = local(patch1, done[:3], some[:3], theirs, (3,))
        done = [*weights, *done[3:], *some[3:]]
        whole = [o.reshape(a.shape) for o, a in zip(done[:3], arrays[3:6], strict=True)]
        return (*whole, *done[3:])

    all_of, part = P(None, None, None), P(None, "dp", None)
    return jax.shard_map(
        whole_step,
        mesh=mesh,
        in_specs=(P(("rep", "dp"), None, None, None),) * 3 + (all_of,) * 3 + (part,) * 6,
        out_specs=(P("rep", None, None),) * 3 + (P("rep", "dp", None),) * 6,
        check_vma=False,
    )
```

profile of v0, /device:TPU:0, one launch (start us, length us, event | category | flops | bytes accessed | tf_op | source)
XLA Modules:
  0.0 241.3 jit_solution(14273358599154324536)
XLA Ops:
  0.6 203.9 %step.1 = (bf16[2,2,2,2,2,64,2816]{6,5,4,3,2,1,0:T(8,128)(2,1)S(1)}, bf16[2,2,2,2,2,64,2816]{6,5,4,3,2,1,0:T(8,128)(2,1)S(1)}, bf16[2,2,2,2,2,176,1024]{6,5,4,3,...) custom-call(bf16[2,2,2,2,2,64,2816]{6,5,4,3,2,1,0:T(8,128)(2,1)} %bi, ...), custom_call_target="tpu_custom_call" | custom-call | tf_op jit(solution)/shard_map/step/pallas_call | solution.py:503
  204.6 1.5 collective-permute-start
  206.1 1.5 collective-permute-start.4
  207.6 0.5 collective-permute-start.5
  208.2 5.5 %collective-permute-start.1 = (bf16[2,64,2816]{2,1,0:T(8,128)(2,1)}, bf16[2,64,2816]{2,1,0:T(8,128)(2,1)S(1)}, u32[]{:S(2)}, u32[]{:S(2)}) collective-permute-start(bf16[2,64,2816]{2,1,0:T(8,128)(2,1)} %get-tuple-element.62), channel_id=1, source_target_pairs={{0,1},{1,0},{2,3},{3,2},{4,5},{5,4},{6,7},{7,6},{8,9},{9,8},{10,11... | collective-permute-start | bytes 2162696 | tf_op jit(solution)/shard_map/ppermute | solution.py:521
  213.6 0.0 collective-permute-start.2
  213.6 6.0 %collective-permute-done.refs_5_ = bf16[2,176,1024]{2,1,0:T(8,128)(2,1)S(1)} collective-permute-done((bf16[2,176,1024]{2,1,0:T(8,128)(2,1)}, bf16[2,176,1024]{2,1,0:T(8,128)(2,1)S(1)}, u32[]{:S(2)}, u32[]{:S(2)}) %collective-permute-start) | collective-permute-done | bytes 720928 | tf_op jit(solution)/shard_map/ppermute | solution.py:518
  219.6 4.7 %collective-permute-start.3 = (bf16[2,176,1024]{2,1,0:T(8,128)(2,1)}, bf16[2,176,1024]{2,1,0:T(8,128)(2,1)S(1)}, u32[]{:S(2)}, u32[]{:S(2)}) collective-permute-start(bf16[2,176,1024]{2,1,0:T(8,128)(2,1)} %get-tuple-element.64), channel_id=1, source_target_pairs={{0,1},{1,0},{2,3},{3,2},{4,5},{5,4},{6,7},{7,6},{8,9},{9,8},{10,11... | collective-permute-start | bytes 2162696 | tf_op jit(solution)/shard_map/ppermute | solution.py:521
  224.3 10.7 %shard_map.187 = (bf16[2,2,2,2,2,64,2816]{6,5,4,3,2,1,0:T(8,128)(2,1)}, bf16[2,2,2,2,2,64,2816]{6,5,4,3,2,1,0:T(8,128)(2,1)}, bf16[2,2,2,2,2,176,1024]{6,5,4,3,2...) custom-call(bf16[2,2,2,2,2,64,2816]{6,5,4,3,2,1,0:T(8,128)(2,1)S(1)} %get-tuple-element., ...), custom_call_target="tpu_custom_call" | custom-call | flops 200000000 | bytes 64000000 | tf_op jit(solution)/shard_map/pallas_call | solution.py:481
  235.0 0.0 collective-permute-done.4.refs_3_
  235.0 0.0 collective-permute-done.5.refs_4_
  235.0 0.0 collective-permute-start.7
  235.1 0.5 collective-permute-start.6
  235.6 0.0 collective-permute-done.1.refs_3_
  235.6 0.0 collective-permute-done.2.refs_4_
  235.6 0.0 collective-permute-done.3.refs_5_
  235.6 1.4 shard_map.188
  237.0 0.1 collective-permute-start.8
  237.1 2.8 %shard_map.189 = (bf16[2,2,2,2,2,64,2816]{6,5,4,3,2,1,0:T(8,128)(2,1)}, bf16[2,2,2,2,2,64,2816]{6,5,4,3,2,1,0:T(8,128)(2,1)}, bf16[2,2,2,2,2,176,1024]{6,5,4,3,2...) custom-call(bf16[2,2,2,2,2,64,2816]{6,5,4,3,2,1,0:T(8,128)(2,1)} %ge, ...), custom_call_target="tpu_custom_call", output_to_operand_aliasing={{0}: (0, {}), {1}: (1, {}), {2}: (2, {})} | custom-call | tf_op jit(solution)/shard_map/pallas_call | solution.py:481
  239.9 0.0 collective-permute-done.7.refs_4_
  239.9 0.0 collective-permute-done.6.refs_3_
  239.9 0.0 collective-permute-done.8.refs_5_
  239.9 1.4 shard_map.190
Async XLA Ops:
  204.6 15.0 %collective-permute-start = (bf16[2,176,1024]{2,1,0:T(8,128)(2,1)}, bf16[2,176,1024]{2,1,0:T(8,128)(2,1)S(1)}, u32[]{:S(2)}, u32[]{:S(2)}) collective-permute-start(bf16[2,176,1024]{2,1,0:T(8,128)(2,1)} %get-tuple-element.50), channel_id=1, source_target_pairs={{0,2},{1,3},{2,0},{3,1},{4,6},{5,7},{6,4},{7,5},{8,10},{9,11},{10,... | collective-permute-start | bytes 2162696 | tf_op jit(solution)/shard_map/ppermute | solution.py:518
  206.1 28.9 %collective-permute-start.4 = (bf16[2,64,2816]{2,1,0:T(8,128)(2,1)}, bf16[2,64,2816]{2,1,0:T(8,128)(2,1)S(1)}, u32[]{:S(2)}, u32[]{:S(2)}) collective-permute-start(bf16[2,64,2816]{2,1,0:T(8,128)(2,1)} %get-tuple-element.69), channel_id=1, source_target_pairs={{0,8},{1,9},{2,10},{3,11},{4,12},{5,13},{6,14},{7,15},{8,0},{9,1},... | collective-permute-start | bytes 2162696 | tf_op jit(solution)/shard_map/ppermute | solution.py:518
  207.6 27.4 %collective-permute-start.5 = (bf16[2,64,2816]{2,1,0:T(8,128)(2,1)}, bf16[2,64,2816]{2,1,0:T(8,128)(2,1)S(1)}, u32[]{:S(2)}, u32[]{:S(2)}) collective-permute-start(bf16[2,64,2816]{2,1,0:T(8,128)(2,1)} %get-tuple-element.72), channel_id=1, source_target_pairs={{0,4},{1,5},{2,6},{3,7},{4,0},{5,1},{6,2},{7,3},{8,12},{9,13},{10,... | collective-permute-start | bytes 2162696 | tf_op jit(solution)/shard_map/ppermute | solution.py:518
  208.2 27.4 %collective-permute-start.1 = (bf16[2,64,2816]{2,1,0:T(8,128)(2,1)}, bf16[2,64,2816]{2,1,0:T(8,128)(2,1)S(1)}, u32[]{:S(2)}, u32[]{:S(2)}) collective-permute-start(bf16[2,64,2816]{2,1,0:T(8,128)(2,1)} %get-tuple-element.62), channel_id=1, source_target_pairs={{0,1},{1,0},{2,3},{3,2},{4,5},{5,4},{6,7},{7,6},{8,9},{9,8},{10,11... | collective-permute-start | bytes 2162696 | tf_op jit(solution)/shard_map/ppermute | solution.py:521
  213.6 21.9 %collective-permute-start.2 = (bf16[2,64,2816]{2,1,0:T(8,128)(2,1)}, bf16[2,64,2816]{2,1,0:T(8,128)(2,1)S(1)}, u32[]{:S(2)}, u32[]{:S(2)}) collective-permute-start(bf16[2,64,2816]{2,1,0:T(8,128)(2,1)} %get-tuple-element.63), channel_id=1, source_target_pairs={{0,1},{1,0},{2,3},{3,2},{4,5},{5,4},{6,7},{7,6},{8,9},{9,8},{10,11... | collective-permute-start | bytes 2162696 | tf_op jit(solution)/shard_map/ppermute | solution.py:521
  219.6 16.0 %collective-permute-start.3 = (bf16[2,176,1024]{2,1,0:T(8,128)(2,1)}, bf16[2,176,1024]{2,1,0:T(8,128)(2,1)S(1)}, u32[]{:S(2)}, u32[]{:S(2)}) collective-permute-start(bf16[2,176,1024]{2,1,0:T(8,128)(2,1)} %get-tuple-element.64), channel_id=1, source_target_pairs={{0,1},{1,0},{2,3},{3,2},{4,5},{5,4},{6,7},{7,6},{8,9},{9,8},{10,11... | collective-permute-start | bytes 2162696 | tf_op jit(solution)/shard_map/ppermute | solution.py:521
  235.0 4.8 %collective-permute-start.7 = (bf16[2,64,2816]{2,1,0:T(8,128)(2,1)S(1)}, bf16[2,64,2816]{2,1,0:T(8,128)(2,1)S(1)}, u32[]{:S(2)}, u32[]{:S(2)}) collective-permute-start(bf16[2,64,2816]{2,1,0:T(8,128)(2,1)S(1)} %collective-permute-done.5.refs_4_), channel_id=1, source_target_pairs={{0,1},{1,0},{2,3},{3,2},{4,5},{5,4},{6,7},{7,6},{8,9},{9,8},{10,11... | collective-permute-start | bytes 2162696 | tf_op jit(solution)/shard_map/ppermute | solution.py:521
  235.1 4.8 %collective-permute-start.6 = (bf16[2,64,2816]{2,1,0:T(8,128)(2,1)S(1)}, bf16[2,64,2816]{2,1,0:T(8,128)(2,1)S(1)}, u32[]{:S(2)}, u32[]{:S(2)}) collective-permute-start(bf16[2,64,2816]{2,1,0:T(8,128)(2,1)S(1)} %collective-permute-done.4.refs_3_), channel_id=1, source_target_pairs={{0,1},{1,0},{2,3},{3,2},{4,5},{5,4},{6,7},{7,6},{8,9},{9,8},{10,11... | collective-permute-start | bytes 2162696 | tf_op jit(solution)/shard_map/ppermute | solution.py:521
  237.0 2.9 %collective-permute-start.8 = (bf16[2,176,1024]{2,1,0:T(8,128)(2,1)S(1)}, bf16[2,176,1024]{2,1,0:T(8,128)(2,1)S(1)}, u32[]{:S(2)}, u32[]{:S(2)}) collective-permute-start(bf16[2,176,1024]{2,1,0:T(8,128)(2,1)S(1)} %collective-permute-done.refs_5_), channel_id=1, source_target_pairs={{0,1},{1,0},{2,3},{3,2},{4,5},{5,4},{6,7},{7,6},{8,9},{9,8},{10,11... | collective-permute-start | bytes 2162696 | tf_op jit(solution)/shard_map/ppermute | solution.py:521
where the time goes:
time: 241 us
  Pallas kernels  220 us (91%)
  starting transfers between devices  14.3 us (6%)
  waiting for transfers between devices  5.98 us (2%)
    pallas_call x1, Pallas kernels, whole_step(): pl.pallas_call(kernel, out_shape=[pltpu.VMEM((*GRID, *s), BF16) for s in...  204 us
    pallas_call x4, Pallas kernels, local(): pl.pallas_call(kernel_, out_shape=[jax.ShapeDtypeStruct(o.shape, o.dtype)...  16.3 us
    ppermute x6, starting transfers between devices, over(): return lax.ppermute(o, 'dp', [(d, d ^ 1) for d in range(16)])  10.8 us
    ppermute x3, waiting for transfers between devices, axis(): lax.ppermute(outs[9 + i], 'dp', [(d, d ^ STRIDES[ORDERS[i][0]]) for d in...  5.96 us
  transfers between devices with their start and end apart: 9, of which 1 were waited for; matrix products, arithmetic and copies ran while one was open for 0% of the time, Pallas kernels for 6%

commit v1 on v0

--- a/solution.py
+++ b/solution.py
@@ -12,6 +12,7 @@
 ORDERS = ((0, 1, 2), (1, 2, 0), (2, 0, 1))
 STRIDES = (8, 4, 2)
 SLAB = 16
+EARLY = 7
 EVERY = slice(None)
 GRID = (LAYERS, 2, 2, 2, 2)
 GRANT = 17 * 1024 * 1024
@@ -430,7 +431,8 @@
 
 
 def put(*refs):
-    ins, outs, sem = refs[:6], refs[6:12], refs[12]
+    half = len(refs) // 2
+    ins, outs, sem = refs[:half], refs[half:-1], refs[-1]
     copies = []
     for i in range(3):
         w = blocks_of(i)
@@ -442,8 +444,9 @@
             (every, *w.block(0, 0, 1), w.core),
         )):
             copies.append(pltpu.make_async_copy(ins[i].at[at], outs[i].at[at], sem.at[i, n]))
+    for j in range(3, half):
         for k in range(LAYERS):
-            copies.append(pltpu.make_async_copy(ins[3 + i].at[k], outs[3 + i].at[k], sem.at[3 + i, k]))
+            copies.append(pltpu.make_async_copy(ins[j].at[k], outs[j].at[k], sem.at[j, k]))
     run(copies)
 
 
@@ -457,12 +460,13 @@
 
 
 def patch0(*refs):
-    _, lates, vs, outs, v_outs = (refs[i : i + 3] for i in range(0, 15, 3))
-    sem = refs[-1]
+    rest = 9 - EARLY
+    lates, vs, outs, v_outs, sem = refs[3:6], refs[6 : 6 + rest], refs[6 + rest : 9 + rest], refs[9 + rest : -1], refs[-1]
     copies = []
     for i in range(3):
         w = blocks_of(i)
         copies.append(pltpu.make_async_copy(lates[i], outs[i].at[(EVERY, *w.far(), w.core)], sem.at[i, 0]))
+    for i in range(rest):
         copies.append(pltpu.make_async_copy(vs[i], v_outs[i], sem.at[i, 1]))
     run(copies)
 
@@ -523,14 +527,14 @@
         late = [axis(i) for i in range(3)]
         mids = [over(o) for o in outs[12:]]
         cost = pl.CostEstimate(flops=PUT_FLOPS, bytes_accessed=2 * 32_000_000, transcendentals=0)
-        done = local(put, outs[:6], [], outs[:6], (6, 3), cost)
+        done = local(put, outs[:EARLY], [], outs[:EARLY], (EARLY, 3), cost)
         for i in range(3):
             late[i], done[3 + i] = lax.optimization_barrier((late[i], done[3 + i]))
         theirs = [over(late[i]) for i in range(2)]
         some = local(patch_mid, done[:3], done[:3], mids, (3,))
         late[2], some[0] = lax.optimization_barrier((late[2], some[0]))
         theirs.append(over(late[2]))
-        some = local(patch0, some + list(outs[6:9]), some, [*late, *outs[6:9]], (3, 2))
+        some = local(patch0, some + list(outs[EARLY:9]), some, [*late, *outs[EARLY:9]], (3, 2))
         weights = local(patch1, done[:3], some[:3], theirs, (3,))
         done = [*weights, *done[3:], *some[3:]]
         whole = [o.reshape(a.shape) for o, a in zip(done[:3], arrays[3:6], strict=True)]

time: 241 us -> 241 us (level)
  no operation moved by 1% of the time
where the time goes in v1:
time: 241 us
  Pallas kernels  220 us (91%)
  starting transfers between devices  14.3 us (6%)
  waiting for transfers between devices  5.98 us (2%)
    pallas_call x1, Pallas kernels, whole_step(): pl.pallas_call(kernel, out_shape=[pltpu.VMEM((*GRID, *s), BF16) for s in...  204 us
    pallas_call x4, Pallas kernels, local(): pl.pallas_call(kernel_, out_shape=[jax.ShapeDtypeStruct(o.shape, o.dtype)...  16.3 us
    ppermute x6, starting transfers between devices, over(): return lax.ppermute(o, 'dp', [(d, d ^ 1) for d in range(16)])  10.8 us
    ppermute x3, waiting for transfers between devices, axis(): lax.ppermute(outs[9 + i], 'dp', [(d, d ^ STRIDES[ORDERS[i][0]]) for d in...  5.96 us
  transfers between devices with their start and end apart: 9, of which 1 were waited for; matrix products, arithmetic and copies ran while one was open for 0% of the time, Pallas kernels for 6%

profile of v1, /device:TPU:0, one launch (start us, length us, event | category | flops | bytes accessed | tf_op | source)
XLA Modules:
  0.0 241.3 jit_solution(7939062296566458661)
XLA Ops:
  0.6 203.9 %step.1 = (bf16[2,2,2,2,2,64,2816]{6,5,4,3,2,1,0:T(8,128)(2,1)S(1)}, bf16[2,2,2,2,2,64,2816]{6,5,4,3,2,1,0:T(8,128)(2,1)S(1)}, bf16[2,2,2,2,2,176,1024]{6,5,4,3,...) custom-call(bf16[2,2,2,2,2,64,2816]{6,5,4,3,2,1,0:T(8,128)(2,1)} %bi, ...), custom_call_target="tpu_custom_call" | custom-call | tf_op jit(solution)/shard_map/step/pallas_call | solution.py:507
  204.6 1.5 collective-permute-start
  206.1 1.5 collective-permute-start.4
  207.6 0.5 collective-permute-start.5
  208.2 5.5 %collective-permute-start.1 = (bf16[2,64,2816]{2,1,0:T(8,128)(2,1)}, bf16[2,64,2816]{2,1,0:T(8,128)(2,1)S(1)}, u32[]{:S(2)}, u32[]{:S(2)}) collective-permute-start(bf16[2,64,2816]{2,1,0:T(8,128)(2,1)} %get-tuple-element.63), channel_id=1, source_target_pairs={{0,1},{1,0},{2,3},{3,2},{4,5},{5,4},{6,7},{7,6},{8,9},{9,8},{10,11... | collective-permute-start | bytes 2162696 | tf_op jit(solution)/shard_map/ppermute | solution.py:525
  213.6 0.0 collective-permute-start.2
  213.6 6.0 %collective-permute-done.refs_5_ = bf16[2,176,1024]{2,1,0:T(8,128)(2,1)S(1)} collective-permute-done((bf16[2,176,1024]{2,1,0:T(8,128)(2,1)}, bf16[2,176,1024]{2,1,0:T(8,128)(2,1)S(1)}, u32[]{:S(2)}, u32[]{:S(2)}) %collective-permute-start) | collective-permute-done | bytes 720928 | tf_op jit(solution)/shard_map/ppermute | solution.py:522
  219.6 4.7 %collective-permute-start.3 = (bf16[2,176,1024]{2,1,0:T(8,128)(2,1)}, bf16[2,176,1024]{2,1,0:T(8,128)(2,1)S(1)}, u32[]{:S(2)}, u32[]{:S(2)}) collective-permute-start(bf16[2,176,1024]{2,1,0:T(8,128)(2,1)} %get-tuple-element.65), channel_id=1, source_target_pairs={{0,1},{1,0},{2,3},{3,2},{4,5},{5,4},{6,7},{7,6},{8,9},{9,8},{10,11... | collective-permute-start | bytes 2162696 | tf_op jit(solution)/shard_map/ppermute | solution.py:525
  224.3 11.2 %shard_map.187 = (bf16[2,2,2,2,2,64,2816]{6,5,4,3,2,1,0:T(8,128)(2,1)}, bf16[2,2,2,2,2,64,2816]{6,5,4,3,2,1,0:T(8,128)(2,1)}, bf16[2,2,2,2,2,176,1024]{6,5,4,3,2...) custom-call(bf16[2,2,2,2,2,64,2816]{6,5,4,3,2,1,0:T(8,128)(2,1)S(1)}, ...), custom_call_target="tpu_custom_call" | custom-call | flops 200000000 | bytes 64000000 | tf_op jit(solution)/shard_map/pallas_call | solution.py:485
  235.5 0.0 collective-permute-done.4.refs_3_
  235.5 0.0 collective-permute-done.5.refs_4_
  235.5 0.0 collective-permute-start.7
  235.5 0.5 collective-permute-start.6
  236.0 0.0 collective-permute-done.1.refs_3_
  236.0 0.0 collective-permute-done.2.refs_4_
  236.0 0.0 collective-permute-done.3.refs_5_
  236.0 1.4 shard_map.188
  237.4 0.1 collective-permute-start.8
  237.5 2.3 shard_map.189
  239.9 0.0 collective-permute-done.7.refs_4_
  239.9 0.0 collective-permute-done.6.refs_3_
  239.9 0.0 collective-permute-done.8.refs_5_
  239.9 1.4 shard_map.190
Async XLA Ops:
  204.6 15.0 %collective-permute-start = (bf16[2,176,1024]{2,1,0:T(8,128)(2,1)}, bf16[2,176,1024]{2,1,0:T(8,128)(2,1)S(1)}, u32[]{:S(2)}, u32[]{:S(2)}) collective-permute-start(bf16[2,176,1024]{2,1,0:T(8,128)(2,1)} %get-tuple-element.50), channel_id=1, source_target_pairs={{0,2},{1,3},{2,0},{3,1},{4,6},{5,7},{6,4},{7,5},{8,10},{9,11},{10,... | collective-permute-start | bytes 2162696 | tf_op jit(solution)/shard_map/ppermute | solution.py:522
  206.1 29.3 %collective-permute-start.4 = (bf16[2,64,2816]{2,1,0:T(8,128)(2,1)}, bf16[2,64,2816]{2,1,0:T(8,128)(2,1)S(1)}, u32[]{:S(2)}, u32[]{:S(2)}) collective-permute-start(bf16[2,64,2816]{2,1,0:T(8,128)(2,1)} %get-tuple-element.70), channel_id=1, source_target_pairs={{0,8},{1,9},{2,10},{3,11},{4,12},{5,13},{6,14},{7,15},{8,0},{9,1},... | collective-permute-start | bytes 2162696 | tf_op jit(solution)/shard_map/ppermute | solution.py:522
  207.6 27.8 %collective-permute-start.5 = (bf16[2,64,2816]{2,1,0:T(8,128)(2,1)}, bf16[2,64,2816]{2,1,0:T(8,128)(2,1)S(1)}, u32[]{:S(2)}, u32[]{:S(2)}) collective-permute-start(bf16[2,64,2816]{2,1,0:T(8,128)(2,1)} %get-tuple-element.73), channel_id=1, source_target_pairs={{0,4},{1,5},{2,6},{3,7},{4,0},{5,1},{6,2},{7,3},{8,12},{9,13},{10,... | collective-permute-start | bytes 2162696 | tf_op jit(solution)/shard_map/ppermute | solution.py:522
  208.2 27.9 %collective-permute-start.1 = (bf16[2,64,2816]{2,1,0:T(8,128)(2,1)}, bf16[2,64,2816]{2,1,0:T(8,128)(2,1)S(1)}, u32[]{:S(2)}, u32[]{:S(2)}) collective-permute-start(bf16[2,64,2816]{2,1,0:T(8,128)(2,1)} %get-tuple-element.63), channel_id=1, source_target_pairs={{0,1},{1,0},{2,3},{3,2},{4,5},{5,4},{6,7},{7,6},{8,9},{9,8},{10,11... | collective-permute-start | bytes 2162696 | tf_op jit(solution)/shard_map/ppermute | solution.py:525
  213.6 22.4 %collective-permute-start.2 = (bf16[2,64,2816]{2,1,0:T(8,128)(2,1)}, bf16[2,64,2816]{2,1,0:T(8,128)(2,1)S(1)}, u32[]{:S(2)}, u32[]{:S(2)}) collective-permute-start(bf16[2,64,2816]{2,1,0:T(8,128)(2,1)} %get-tuple-element.64), channel_id=1, source_target_pairs={{0,1},{1,0},{2,3},{3,2},{4,5},{5,4},{6,7},{7,6},{8,9},{9,8},{10,11... | collective-permute-start | bytes 2162696 | tf_op jit(solution)/shard_map/ppermute | solution.py:525
  219.6 16.4 %collective-permute-start.3 = (bf16[2,176,1024]{2,1,0:T(8,128)(2,1)}, bf16[2,176,1024]{2,1,0:T(8,128)(2,1)S(1)}, u32[]{:S(2)}, u32[]{:S(2)}) collective-permute-start(bf16[2,176,1024]{2,1,0:T(8,128)(2,1)} %get-tuple-element.65), channel_id=1, source_target_pairs={{0,1},{1,0},{2,3},{3,2},{4,5},{5,4},{6,7},{7,6},{8,9},{9,8},{10,11... | collective-permute-start | bytes 2162696 | tf_op jit(solution)/shard_map/ppermute | solution.py:525
  235.5 4.4 %collective-permute-start.7 = (bf16[2,64,2816]{2,1,0:T(8,128)(2,1)S(1)}, bf16[2,64,2816]{2,1,0:T(8,128)(2,1)S(1)}, u32[]{:S(2)}, u32[]{:S(2)}) collective-permute-start(bf16[2,64,2816]{2,1,0:T(8,128)(2,1)S(1)} %collective-permute-done.5.refs_4_), channel_id=1, source_target_pairs={{0,1},{1,0},{2,3},{3,2},{4,5},{5,4},{6,7},{7,6},{8,9},{9,8},{10,11... | collective-permute-start | bytes 2162696 | tf_op jit(solution)/shard_map/ppermute | solution.py:525
  235.5 4.4 %collective-permute-start.6 = (bf16[2,64,2816]{2,1,0:T(8,128)(2,1)S(1)}, bf16[2,64,2816]{2,1,0:T(8,128)(2,1)S(1)}, u32[]{:S(2)}, u32[]{:S(2)}) collective-permute-start(bf16[2,64,2816]{2,1,0:T(8,128)(2,1)S(1)} %collective-permute-done.4.refs_3_), channel_id=1, source_target_pairs={{0,1},{1,0},{2,3},{3,2},{4,5},{5,4},{6,7},{7,6},{8,9},{9,8},{10,11... | collective-permute-start | bytes 2162696 | tf_op jit(solution)/shard_map/ppermute | solution.py:525
  237.4 2.5 %collective-permute-start.8 = (bf16[2,176,1024]{2,1,0:T(8,128)(2,1)S(1)}, bf16[2,176,1024]{2,1,0:T(8,128)(2,1)S(1)}, u32[]{:S(2)}, u32[]{:S(2)}) collective-permute-start(bf16[2,176,1024]{2,1,0:T(8,128)(2,1)S(1)} %collective-permute-done.refs_5_), channel_id=1, source_target_pairs={{0,1},{1,0},{2,3},{3,2},{4,5},{5,4},{6,7},{7,6},{8,9},{9,8},{10,11... | collective-permute-start | bytes 2162696 | tf_op jit(solution)/shard_map/ppermute | solution.py:525
